TPU v7x, 8 devices: a whole 2x2x1 slice. The times are simulated.
8 devices in a mesh: batch: 1 (over z), col: 2 (over y), row: 4 (over x, core).
Axes of the slice: x: 2, y: 2, z: 1, core: 2. Of those that a mesh axis runs over, the one named last changes fastest.
Arguments:
- mat_blocks: float32 [8192, 256, 64], P(('batch', 'row'), 'col')
Outputs:
- output 1: float32 [8192, 256, 64], P(('batch', 'row'), 'col')
- output 2: float32 [256], P('batch')
- output 3: float32 [4, 64, 64], P('batch')
All inputs are finite; a program needn't handle non-finite values.
Results may differ from a plain program's by a relative error of at most 0.001.
Values sent between devices are 32-bit elements.
A program may use at most 1 GiB of HBM per device.

v0:
```python
import math
import jax
import jax.numpy as jnp
from jax import lax
from jax.sharding import PartitionSpec as P

PANELS = 4
HIGHEST = lax.Precision.HIGHEST


def mat_dot(left_mat, right_mat):
    return jnp.dot(left_mat, right_mat, precision=HIGHEST, preferred_element_type=jnp.float32)


def mat_einsum(einsum_form, left_mat, right_mat):
    return jnp.einsum(einsum_form, left_mat, right_mat, precision=HIGHEST, preferred_element_type=jnp.float32)


def apply_reflector(panel_work, tau_vec, column, col_idx, pivot_row, row_ids, tail_dots, pivot_line):
    col_ids = jnp.arange(panel_work.shape[1])
    alpha_val = lax.dynamic_index_in_dim(pivot_line, col_idx, keepdims=False)
    norm_val = jnp.sqrt(lax.dynamic_index_in_dim(tail_dots, col_idx, keepdims=False))
    beta_val = jnp.where(alpha_val >= 0.0, -norm_val, norm_val)
    tau_val = (beta_val - alpha_val) / beta_val
    scale_val = 1.0 / (alpha_val - beta_val)
    refl_vec = jnp.where(row_ids > pivot_row, column * scale_val, jnp.where(row_ids == pivot_row, 1.0, 0.0))
    refl_dot = scale_val * (tail_dots - alpha_val * pivot_line) + pivot_line
    refl_dot = jnp.where(col_ids > col_idx, refl_dot, 0.0)
    new_col = jnp.where(row_ids < pivot_row, column, jnp.where(row_ids == pivot_row, beta_val, refl_vec))
    panel_work = jnp.where(col_ids[None, :] == col_idx, new_col[:, None], panel_work - tau_val * refl_vec[:, None] * refl_dot[None, :])
    tau_vec = jnp.where(col_ids == col_idx, tau_val, tau_vec)
    return panel_work, tau_vec


def factor_panel_rows(panel_in, row_base, pivot_base):
    local_rows, block_width = panel_in.shape
    row_ids = row_base + jnp.arange(local_rows)

    def column_step(col_idx, loop_state):
        panel_work, tau_vec = loop_state
        pivot_row = pivot_base + col_idx
        column = lax.dynamic_index_in_dim(panel_work, col_idx, axis=1, keepdims=False)
        tail_col = jnp.where(row_ids >= pivot_row, column, 0.0)
        local_pivot = jnp.clip(pivot_row - row_base, 0, local_rows - 1)
        holds_pivot = (pivot_row >= row_base) & (pivot_row < row_base + local_rows)
        pivot_line = lax.dynamic_index_in_dim(panel_work, local_pivot, axis=0, keepdims=False)
        pivot_line = jnp.where(holds_pivot, pivot_line, 0.0)
        packed = jnp.concatenate([mat_dot(tail_col[None, :], panel_work)[0], pivot_line])
        packed = lax.psum(packed, 'row')
        return apply_reflector(panel_work, tau_vec, column, col_idx, pivot_row, row_ids, packed[:block_width], packed[block_width:])

    return lax.fori_loop(0, block_width, column_step, (panel_in, jnp.zeros((block_width,), jnp.float32)))


def tfactor_from_gram(gram_mat, tau_vec):
    block_width = gram_mat.shape[0]
    col_ids = jnp.arange(block_width)
    step_mat = -tau_vec[:, None] * jnp.where(col_ids[None, :] > col_ids[:, None], gram_mat, 0.0)
    eye_mat = jnp.eye(block_width, dtype=jnp.float32)
    inv_acc = eye_mat + step_mat
    power_mat = step_mat
    for level_num in range(max(1, math.ceil(math.log2(block_width))) - 1):
        power_mat = mat_dot(power_mat, power_mat)
        inv_acc = mat_dot(inv_acc, eye_mat + power_mat)
    return inv_acc * tau_vec[None, :]


def solution(mesh):
    col_count = mesh.shape['col']
    block_spec = P(('batch', 'row'), 'col', None)

    def device_fn(a_local):
        local_rows, local_blocks, block_width = a_local.shape
        col_rank = lax.axis_index('col')
        row_base = lax.axis_index('row') * local_rows
        row_ids = row_base + jnp.arange(local_rows)
        col_ids = jnp.arange(block_width)
        global_ids = jnp.arange(local_blocks) * col_count + col_rank
        tau_list = []
        tfac_list = []
        for panel_idx in range(PANELS):
            owner_col = panel_idx % col_count
            block_pos = panel_idx // col_count
            pivot_ids = panel_idx * block_width + col_ids
            panel_out, tau_vec = factor_panel_rows(a_local[:, block_pos, :], row_base, panel_idx * block_width)
            refl_mat = jnp.where(row_ids[:, None] > pivot_ids[None, :], panel_out, jnp.where(row_ids[:, None] == pivot_ids[None, :], 1.0, 0.0))
            gram_mat = lax.psum(mat_einsum('rk,rj->kj', refl_mat, refl_mat), 'row')
            t_factor = tfactor_from_gram(gram_mat, tau_vec)
            packed = jnp.concatenate([refl_mat, t_factor], axis=0)
            packed = lax.psum(jnp.where(col_rank == owner_col, packed, 0.0), 'col')
            refl_mat = packed[:local_rows]
            t_factor = packed[local_rows:]
            w_summed = lax.psum(mat_einsum('rk,rbc->kbc', refl_mat, a_local), 'row')
            w_mat = mat_einsum('kj,kbc->jbc', t_factor, w_summed)
            w_mat = jnp.where((global_ids > panel_idx)[None, :, None], w_mat, 0.0)
            a_local = a_local - mat_einsum('rj,jbc->rbc', refl_mat, w_mat)
            a_local = jnp.where((global_ids == panel_idx)[None, :, None], panel_out[:, None, :], a_local)
            tau_list.append(jnp.diagonal(t_factor))
            tfac_list.append(t_factor)
        return a_local, jnp.concatenate(tau_list), jnp.stack(tfac_list)

    return jax.shard_map(device_fn, mesh=mesh, in_specs=(block_spec,), out_specs=(block_spec, P('batch'), P('batch', None, None)), check_vma=False)
```

profile of v0, /device:TPU:0, one launch (start us, length us, event | category | flops | bytes accessed | tf_op | source)
XLA Modules:
  0.0 4074.0 jit_solution(7018654085079340456)
XLA Ops:
  7.2 38.5 copy.41
  45.7 753.8 %while.76 = (s32[]{:T(128)}, f32[2048,64]{0,1:T(8,128)S(1)}, f32[64]{0:T(128)S(1)}, s32[]{:T(128)}, s32[]{:T(128)}, /*index=5*/s32[]{:T(128)}, s32[]{:T(128)}, s32[]{:T(128)}, f32[]{:T(128)}, f32[]{:T(128)}) while((s32[]{:T(128)}, f32[2048,64]{0,1:T(8,128)S(1)}, f32[64]{0:T(128)S(1)}, s32[]{:T(128)}, ...), condition=%wide.region_2.3_spmd.clone.clone.clone, body=%wide.region_0.2_spmd.clone.clone.clone.sunk | while | flops 1995728 | bytes 1672931 | solution.py:52
  813.4 70.4 %copy.27 = f32[2048,128,64]{0,1,2:T(8,128)} copy(f32[2048,128,64]{1,2,0:T(8,128)} %param.9) | data formatting | bytes 134217728 | tf_op args[0]
  883.8 68.6 %fusion.44 = f32[64,128,64]{1,0,2:T(8,128)} fusion(f32[2048,128,64]{0,1,2:T(8,128)} %copy.27, f32[2112,64]{0,1:T(8,128)} %all-reduce.9.cloned.1.call-done), kind=kOutput, calls=%fused_computation.129 | convolution fusion | flops 12884901888 | bytes 69730304 | tf_op jit(solution)/shard_map/rk,rbc->kbc/dot_general | solution.py:16
  952.7 46.3 %all-reduce.11.cloned.1.call-done = f32[64,128,64]{1,0,2:T(8,128)} async-done(((f32[64,128,64]{1,0,2:T(8,128)}), f32[64,128,64]{1,0,2:T(8,128)}) %all-reduce.11.cloned.1.call-update) | async-done | bytes 2097168 | tf_op jit(solution)/shard_map/psum | solution.py:93
  1002.5 64.0 %subtract_select_fusion.7 = f32[2048,128,64]{0,1,2:T(8,128)} fusion(f32[2048,128,64]{0,1,2:T(8,128)} %copy.27, f32[2048,64]{0,1:T(8,128)S(1)} %get-tuple-element.483, pred[128]{0:T(512)(128)(4,1)S(1)} %get-tuple-element.812, f32[64,128,64]{1,0,2:T(8,128)S(1)} %fusion.70, pred[128]{0:T(512)(128)(4,1)S(1)} %get-tuple-element.811, f32[2112,64]{0,1:T(8,128)S(1)} %copy-done), kind=kOutput, calls=%fused_computation.91 | convolution fusion | flops 12918980608 | bytes 137364480 | tf_op jit(solution)/shard_map/rj,jbc->rbc/dot_general | solution.py:16
  1069.2 755.7 %while.77 = (s32[]{:T(128)}, f32[2048,64]{0,1:T(8,128)S(1)}, f32[64]{0:T(128)S(1)}, s32[]{:T(128)}, s32[]{:T(128)}, /*index=5*/s32[]{:T(128)}, s32[]{:T(128)}, s...) while((s32[]{:T(128)}, f32[2048,64]{0,1:T(8,128)S(1)}, f32[64]{0:T(128)S(1)}, ...), condition=%wide.region_8.9_spmd.clone.clone.clone, body=%wide.region_6.8_spmd.clone.clone.clone.sunk | while | flops 1995729 | bytes 1672951 | solution.py:52
  1825.6 11.3 psum.135
  1839.7 23.7 all-reduce.13.cloned.1.call-done
  1863.5 68.6 %fusion.45 = f32[64,128,64]{1,0,2:T(8,128)} fusion(f32[2048,128,64]{0,1,2:T(8,128)} %subtract_select_fusion.7, f32[2112,64]{0,1:T(8,128)} %all-reduce.13.cloned.1.call-done), kind=kOutput, calls=%fused_computation.130 | convolution fusion | flops 12884901888 | bytes 69730304 | tf_op jit(solution)/shard_map/rk,rbc->kbc/dot_general | solution.py:16
  1932.6 45.3 %all-reduce.15.cloned.1.call-done = f32[64,128,64]{1,0,2:T(8,128)} async-done(((f32[64,128,64]{1,0,2:T(8,128)}), f32[64,128,64]{1,0,2:T(8,128)}) %all-reduce.15.cloned.1.call-update) | async-done | bytes 2097168 | tf_op jit(solution)/shard_map/psum | solution.py:93
  1981.4 64.0 %subtract_select_fusion.6 = f32[2048,128,64]{0,1,2:T(8,128)} fusion(f32[2048,128,64]{0,1,2:T(8,128)} %subtract_select_fusion.7, f32[2048,64]{0,1:T(8,128)S(1)} %get-tuple-element.485, pred[128]{0:T(512)(128)(4,1)S(1)} %get-tuple-element.814, f32[64,128,64]{1,0,2:T(8,128)S(1)} %fusion.68, pred[128]{0:T(512)(128)(4,1)S(1)} %get-tuple-element.813, ...), kind=kOutput, calls=%fused_computation.90 | convolution fusion | flops 12918980608 | bytes 137364480 | tf_op jit(solution)/shard_map/rj,jbc->rbc/dot_general | solution.py:16
  2048.3 755.6 %while.78 = (s32[]{:T(128)}, f32[2048,64]{0,1:T(8,128)S(1)}, f32[64]{0:T(128)S(1)}, s32[]{:T(128)}, s32[]{:T(128)}, /*index=5*/s32[]{:T(128)}, s32[]{:T(128)}, s...) while((s32[]{:T(128)}, f32[2048,64]{0,1:T(8,128)S(1)}, ...), condition=%wide.region_14.15_spmd.clone.clone.clone, body=%wide.region_12.14_spmd.clone.clone.clone.sunk | while | flops 1995729 | bytes 1672951 | solution.py:52
  2818.7 23.7 all-reduce.17.cloned.1.call-done
  2842.4 68.6 %fusion.46 = f32[64,128,64]{1,0,2:T(8,128)} fusion(f32[2048,128,64]{0,1,2:T(8,128)} %subtract_select_fusion.6, f32[2112,64]{0,1:T(8,128)} %all-reduce.17.cloned.1.call-done), kind=kOutput, calls=%fused_computation.131 | convolution fusion | flops 12884901888 | bytes 69730304 | tf_op jit(solution)/shard_map/rk,rbc->kbc/dot_general | solution.py:16
  2911.3 45.5 %all-reduce.19.cloned.1.call-done = f32[64,128,64]{1,0,2:T(8,128)} async-done(((f32[64,128,64]{1,0,2:T(8,128)}), f32[64,128,64]{1,0,2:T(8,128)}) %all-reduce.19.cloned.1.call-update) | async-done | bytes 2097168 | tf_op jit(solution)/shard_map/psum | solution.py:93
  2960.3 64.0 %subtract_select_fusion.5 = f32[2048,128,64]{0,1,2:T(8,128)} fusion(f32[2048,128,64]{0,1,2:T(8,128)} %subtract_select_fusion.6, f32[2048,64]{0,1:T(8,128)S(1)} %get-tuple-element.487, pred[128]{0:T(512)(128)(4,1)S(1)} %get-tuple-element.818, f32[64,128,64]{1,0,2:T(8,128)S(1)} %fusion.66, pred[128]{0:T(512)(128)(4,1)S(1)} %get-tuple-element.817, ...), kind=kOutput, calls=%fused_computation.89 | convolution fusion | flops 12918980608 | bytes 137364480 | tf_op jit(solution)/shard_map/rj,jbc->rbc/dot_general | solution.py:16
  3027.2 755.7 %while.79 = (s32[]{:T(128)}, f32[2048,64]{0,1:T(8,128)S(1)}, f32[64]{0:T(128)S(1)}, s32[]{:T(128)}, s32[]{:T(128)}, /*index=5*/s32[]{:T(128)}, s32[]{:T(128)}, s...) while((s32[]{:T(128)}, f32[2048,64]{0,1:T(8,128)S(1)}, ...), condition=%wide.region_20.21_spmd.clone.clone.clone, body=%wide.region_18.20_spmd.clone.clone.clone.sunk | while | flops 1995729 | bytes 1672951 | solution.py:52
  3783.6 11.3 psum.141
  3797.8 23.7 all-reduce.21.cloned.1.call-done
  3821.5 68.6 %fusion.47 = f32[64,128,64]{1,0,2:T(8,128)} fusion(f32[2048,128,64]{0,1,2:T(8,128)} %subtract_select_fusion.5, f32[2112,64]{0,1:T(8,128)} %all-reduce.21.cloned.1.call-done), kind=kOutput, calls=%fused_computation.132 | convolution fusion | flops 12884901888 | bytes 69730304 | tf_op jit(solution)/shard_map/rk,rbc->kbc/dot_general | solution.py:16
  3895.6 40.3 all-reduce.23.cloned.1.call-done
  3939.4 64.3 %subtract_select_fusion.4 = f32[2048,128,64]{0,1,2:T(8,128)} fusion(f32[2048,128,64]{0,1,2:T(8,128)} %subtract_select_fusion.5, f32[2048,64]{0,1:T(8,128)S(1)} %get-tuple-element.489, pred[128]{0:T(512)(128)(4,1)S(1)} %get-tuple-element.816, f32[64,128,64]{1,0,2:T(8,128)S(1)} %fusion.64, pred[128]{0:T(512)(128)(4,1)S(1)} %get-tuple-element.815, ...), kind=kOutput, calls=%fused_computation.88 | convolution fusion | flops 12918980608 | bytes 137364480 | tf_op jit(solution)/shard_map/rj,jbc->rbc/dot_general | solution.py:16
  4003.7 63.3 %copy.32 = f32[2048,128,64]{1,2,0:T(8,128)} copy(f32[2048,128,64]{0,1,2:T(8,128)} %subtract_select_fusion.4) | data formatting | bytes 134217728
  (3957 shorter events, 2368.9 us)
Async XLA Ops:
  7.2 876.7 %all-reduce.9.cloned.1.call-start = ((), (), s32[]{:S(2)}) async-start(), calls=%async_computation | async-start | bytes 1114112 | tf_op jit(solution)/shard_map/psum | solution.py:90
  813.4 185.6 %all-reduce.11.cloned.1.call-start = ((), (), s32[]{:S(2)}) async-start(), calls=%async_computation.1 | async-start | bytes 4194304 | tf_op jit(solution)/shard_map/psum | solution.py:93
  952.4 46.6 %copy-start = (f32[2112,64]{0,1:T(8,128)S(1)}, f32[2112,64]{0,1:T(8,128)}, u32[]{:S(2)}) copy-start(f32[2112,64]{0,1:T(8,128)} %all-reduce.9.cloned.1.call-done) | copy-start | bytes 1622020
  952.4 911.0 %all-reduce.13.cloned.1.call-start = ((), (), s32[]{:S(2)}) async-start(), calls=%async_computation.2 | async-start | bytes 1114112 | tf_op jit(solution)/shard_map/psum | solution.py:90
  1839.7 138.2 %all-reduce.15.cloned.1.call-start = ((), (), s32[]{:S(2)}) async-start(), calls=%async_computation.3 | async-start | bytes 4194304 | tf_op jit(solution)/shard_map/psum | solution.py:93
  1932.0 45.8 %copy-start.1 = (f32[2112,64]{0,1:T(8,128)S(1)}, f32[2112,64]{0,1:T(8,128)}, u32[]{:S(2)}) copy-start(f32[2112,64]{0,1:T(8,128)} %all-reduce.13.cloned.1.call-done) | copy-start | bytes 1622020
  1932.1 910.3 %all-reduce.17.cloned.1.call-start = ((), (), s32[]{:S(2)}) async-start(), calls=%async_computation.4 | async-start | bytes 1114112 | tf_op jit(solution)/shard_map/psum | solution.py:90
  2818.6 138.2 %all-reduce.19.cloned.1.call-start = ((), (), s32[]{:S(2)}) async-start(), calls=%async_computation.5 | async-start | bytes 4194304 | tf_op jit(solution)/shard_map/psum | solution.py:93
  2910.9 45.8 %copy-start.2 = (f32[2112,64]{0,1:T(8,128)S(1)}, f32[2112,64]{0,1:T(8,128)}, u32[]{:S(2)}) copy-start(f32[2112,64]{0,1:T(8,128)} %all-reduce.17.cloned.1.call-done) | copy-start | bytes 1622020
  2911.0 910.5 %all-reduce.21.cloned.1.call-start = ((), (), s32[]{:S(2)}) async-start(), calls=%async_computation.6 | async-start | bytes 1114112 | tf_op jit(solution)/shard_map/psum | solution.py:90
  3797.7 138.2 %all-reduce.23.cloned.1.call-start = ((), (), s32[]{:S(2)}) async-start(), calls=%async_computation.7 | async-start | bytes 4194304 | tf_op jit(solution)/shard_map/psum | solution.py:93
  3890.1 3.3 copy-start.3
Sparse Core Ops, SparseCore 0:
  813.5 24.3 all-reduce.8
  952.6 46.4 all-reduce.10
  1839.8 23.6 all-reduce.12
  1932.2 45.6 all-reduce.14
  2818.7 23.5 all-reduce.16
  2911.1 45.6 all-reduce.18
  3797.9 23.6 all-reduce.20
  3890.2 45.6 all-reduce.22
where the time goes:
time: 4100 us; the launch traced here: 4070 us
  blocking collectives  1570 us (38%)
  loops' own time  716 us (17%)
  matrix products  685 us (17%)
  local copies, waits for them, and re-layouts  519 us (13%)
  other arithmetic  318 us (8%)
  waiting for transfers between devices  249 us (6%)
    psum x256, blocking collectives, column_step(): packed = lax.psum(packed, 'row')  1530 us
    another operation x4, loops' own time, factor_panel_rows(): lax.fori_loop(0, block_width, column_step, (panel_in, jnp.zeros((block_wi...  716 us
    dot_general x16, matrix products, mat_einsum(): jnp.einsum(einsum_form, left_mat, right_mat, precision=HIGHEST, preferred...  547 us
    select_n x256, other arithmetic, apply_reflector(): refl_dot = jnp.where(col_ids > col_idx, refl_dot, 0.0)  190 us
    psum x4, waiting for transfers between devices, device_fn(): w_summed = lax.psum(mat_einsum('rk,rbc->kbc', refl_mat, a_local), 'row')  177 us
    unnamed x15, local copies, waits for them, and re-layouts  173 us
    dynamic_slice x256, local copies, waits for them, and re-layouts, apply_reflector(): alpha_val = lax.dynamic_index_in_dim(pivot_line, col_idx, keepdims=False)  162 us
    dynamic_slice x256, local copies, waits for them, and re-layouts, apply_reflector(): lax.dynamic_index_in_dim(tail_dots, col_idx, keepdims=False)  148 us
  transfers between devices with their start and end apart: 8, of which 7 were waited for; matrix products, arithmetic and copies ran while one was open for 2% of the time, Pallas kernels for 0%

commit v1 on v0

v1 whole, which is shorter than its diff:
```python
import jax
import jax.numpy as jnp
from jax import lax
from jax.experimental import pallas as pl
from jax.experimental.pallas import tpu as pltpu
from jax.sharding import PartitionSpec as P

NB = 64
LANES = 128
PANELS = 4
WIDTH = NB * PANELS
HIGHEST = lax.Precision.HIGHEST


def split3(x):
    high = x.astype(jnp.bfloat16)
    rest = x - high.astype(jnp.float32)
    mid = rest.astype(jnp.bfloat16)
    low = (rest - mid.astype(jnp.float32)).astype(jnp.bfloat16)
    return high, mid, low


def small_dot(a, b):
    return jnp.dot(a, b, precision=HIGHEST, preferred_element_type=jnp.float32)


def factor_panel(panel, src_ref, out_ref, vs_ref, st_ref, h_ref):
    n_tiles = src_ref.shape[0]
    base = panel * NB
    lane = lax.broadcasted_iota(jnp.int32, (8, LANES), 1)
    sub = lax.broadcasted_iota(jnp.int32, (8, LANES), 0)
    groups = NB // 8
    zero = jnp.zeros((8, LANES), jnp.float32)

    def tile(g, t):
        return (t, pl.ds(base + 8 * g, 8), slice(None))

    def splat(v):
        return jnp.broadcast_to(jnp.sum(v, axis=1, keepdims=True), (8, LANES))

    def row(ref, j, t):
        return ref[t, pl.ds(base + j, 8, stride=0), :]

    def finish(acc, piv, accn, alf):
        return [splat(a) for a in acc], [splat(a) for a in piv], splat(accn), splat(alf)

    def start():
        acc = [zero] * groups
        piv = [zero] * groups
        accn = zero
        alf = zero
        for t in range(n_tiles):
            x = row(src_ref, 0, t)
            if t < 2:
                rid = lane + t * LANES
                alf = alf + jnp.where(rid == base, x, 0.0)
                x = jnp.where(rid > base, x, 0.0)
            accn = accn + x * x
            for g in range(groups):
                a = src_ref[tile(g, t)]
                if src_ref is not out_ref:
                    out_ref[tile(g, t)] = a
                if t < 2:
                    piv[g] = piv[g] + jnp.where(rid == base, a, 0.0)
                acc[g] = acc[g] + x * a
        return finish(acc, piv, accn, alf)

    carry = start()
    for g0 in range(groups):
        n_g = groups - g0

        def step(s, carry, g0=g0, n_g=n_g):
            (dots, pivs, norm2, alpha), coef = carry
            j = g0 * 8 + s
            k = base + j
            norm = jnp.sqrt(alpha * alpha + norm2)
            beta = jnp.where(alpha >= 0.0, -norm, norm)
            tau = (beta - alpha) / beta
            scale = 1.0 / (alpha - beta)
            coef = [jnp.where(sub == s, new, old) for new, old in zip((tau, scale, beta), coef)]
            hs, fs = [], []
            for i in range(n_g):
                f = tau * (scale * dots[i] + pivs[i])
                if i == 0:
                    f = jnp.where(sub > s, f, 0.0)
                h = f * scale
                h_ref[pl.ds(8 * (g0 + i), 8), :] = h
                h_ref[pl.ds(NB + 8 * (g0 + i), 8), :] = f
                hs.append(h)
                fs.append(f)
            j1 = jnp.minimum(j + 1, NB - 1)
            k1 = k + 1
            h1 = h_ref[pl.ds(j1, 8, stride=0), :]
            f1 = h_ref[pl.ds(NB + j1, 8, stride=0), :]
            acc = [zero] * n_g
            piv = [zero] * n_g
            accn = zero
            alf = zero
            for t in range(n_tiles):
                x = row(out_ref, j, t)
                x1 = row(out_ref, j1, t)
                if t < 2:
                    rid = lane + t * LANES
                    xm = jnp.where(rid > k, x, 0.0)
                    pm = jnp.where(rid == k, 1.0, 0.0)
                    x1 = x1 - h1 * xm - f1 * pm
                    alf = alf + jnp.where(rid == k1, x1, 0.0)
                    x1 = jnp.where(rid > k1, x1, 0.0)
                else:
                    x1 = x1 - h1 * x
                accn = accn + x1 * x1
                for i in range(n_g):
                    a = out_ref[tile(g0 + i, t)]
                    if t < 2:
                        a = a - hs[i] * xm - fs[i] * pm
                        piv[i] = piv[i] + jnp.where(rid == k1, a, 0.0)
                    else:
                        a = a - hs[i] * x
                    out_ref[tile(g0 + i, t)] = a
                    acc[i] = acc[i] + x1 * a
            return finish(acc, piv, accn, alf), coef

        carry, coef = lax.fori_loop(0, 8, step, (carry, [zero] * 3))
        for i in range(3):
            st_ref[i, pl.ds(8 * g0, 8), :] = coef[i]
        dots, pivs, norm2, alpha = carry
        carry = (dots[1:], pivs[1:], norm2, alpha)

    lane16 = lax.broadcasted_iota(jnp.int32, (16, LANES), 1)
    sub16 = lax.broadcasted_iota(jnp.int32, (16, LANES), 0)
    for g in range(groups // 2):
        scale = st_ref[1, pl.ds(16 * g, 16), :]
        beta = st_ref[2, pl.ds(16 * g, 16), :]
        kk = base + 16 * g + sub16
        place = pl.ds(base + 16 * g, 16)
        for t in range(n_tiles):
            a = out_ref[t, place, :]
            v = a * scale
            full = v
            if t < 2:
                rid = lane16 + t * LANES
                full = jnp.where(rid > kk, v, jnp.where(rid == kk, beta, a))
                v = jnp.where(rid > kk, v, jnp.where(rid == kk, 1.0, 0.0))
            out_ref[t, place, :] = full
            for i, part in enumerate(split3(v)):
                vs_ref[i, t, place, :] = part


def panel_dots(load_lhs, rows, panel, vs_ref, acc_ref, n_tiles):
    step_tiles = 8
    acc_ref[pl.ds(0, rows), :] = jnp.zeros((rows, NB), jnp.float32)

    def body(chunk, _):
        parts = [load_lhs(chunk * step_tiles + i) for i in range(step_tiles)]
        lhs = jnp.concatenate([jnp.concatenate([p[s] for p in parts], axis=1) for s in range(3)], axis=0)
        rhs = jnp.concatenate(
            [
                jnp.concatenate(
                    [vs_ref[s, chunk * step_tiles + i, pl.ds(panel * NB, NB), :] for i in range(step_tiles)], axis=1
                )
                for s in range(3)
            ],
            axis=0,
        )
        prod = lax.dot_general(lhs, rhs, (((1,), (1,)), ((), ())), preferred_element_type=jnp.float32)
        top, mid, low = prod[:rows], prod[rows : 2 * rows], prod[2 * rows :]
        small = (top[:, 2 * NB :] + low[:, :NB]) + mid[:, NB : 2 * NB]
        acc_ref[pl.ds(0, rows), :] += (small + (top[:, NB : 2 * NB] + mid[:, :NB])) + top[:, :NB]
        return 0

    lax.fori_loop(0, n_tiles // step_tiles, body, 0)
    return acc_ref[pl.ds(0, rows), :]


def t_from_gram(gram, tau_rows):
    ii = lax.broadcasted_iota(jnp.int32, (NB, NB), 0)
    jj = lax.broadcasted_iota(jnp.int32, (NB, NB), 1)
    eye = jnp.where(ii == jj, 1.0, 0.0)
    power = jnp.where(jj > ii, -tau_rows * gram, 0.0)
    inv = eye + power
    for _ in range(5):
        power = small_dot(power, power)
        inv = inv + small_dot(inv, power)
    tau_cols = jnp.sum(jnp.where(ii == jj, tau_rows, 0.0), axis=0, keepdims=True)
    return inv * tau_cols


def factor_all_kernel(p_ref, out_ref, vs_ref, t_ref, tfull_ref, st_ref, h_ref, acc_ref):
    n_tiles = p_ref.shape[0]
    tfull_ref[...] = jnp.zeros_like(tfull_ref)
    for panel in range(PANELS):
        src = p_ref if panel == 0 else out_ref
        factor_panel(panel, src, out_ref, vs_ref, st_ref, h_ref)
        seen = NB * (panel + 1)
        gram = panel_dots(
            lambda t: [vs_ref[s, t, pl.ds(0, seen), :] for s in range(3)], seen, panel, vs_ref, acc_ref, n_tiles
        )
        t_mat = t_from_gram(gram[seen - NB :], st_ref[0][:, :NB])
        t_ref[panel] = t_mat
        here = pl.ds(seen - NB, NB)
        tfull_ref[here, here] = t_mat
        if panel:
            before = pl.ds(0, seen - NB)
            cross = small_dot(tfull_ref[before, before], gram[: seen - NB])
            tfull_ref[before, here] = -small_dot(cross, t_mat)
        if panel == PANELS - 1:
            break
        left = WIDTH - seen
        rest = pl.ds(seen, left)
        w_sum = panel_dots(lambda t: split3(src[t, rest, :]), left, panel, vs_ref, acc_ref, n_tiles)
        high, mid, low = split3(small_dot(w_sum, t_mat))
        lhs = jnp.concatenate([high, high, high, mid, mid, low], axis=1)

        def body(pair, _):
            tiles = (2 * pair, 2 * pair + 1)
            rhs = jnp.concatenate(
                [
                    jnp.concatenate([vs_ref[s, t, pl.ds(panel * NB, NB), :] for t in tiles], axis=1)
                    for s in (0, 1, 2, 0, 1, 0)
                ],
                axis=0,
            )
            prod = jnp.dot(lhs, rhs, preferred_element_type=jnp.float32)
            for i, t in enumerate(tiles):
                out_ref[t, rest, :] = src[t, rest, :] - prod[:, i * LANES : (i + 1) * LANES]
            return 0

        lax.fori_loop(0, n_tiles // 2, body, 0)


def factor_all(panels):
    n_tiles = panels.shape[0]
    vmem = pl.BlockSpec(memory_space=pltpu.VMEM)
    return pl.pallas_call(
        factor_all_kernel,
        out_shape=(
            jax.ShapeDtypeStruct(panels.shape, jnp.float32),
            jax.ShapeDtypeStruct((3, *panels.shape), jnp.bfloat16),
            jax.ShapeDtypeStruct((PANELS, NB, NB), jnp.float32),
            jax.ShapeDtypeStruct((WIDTH, WIDTH), jnp.float32),
        ),
        in_specs=[vmem],
        out_specs=[vmem] * 4,
        scratch_shapes=[
            pltpu.VMEM((3, NB, LANES), jnp.float32),
            pltpu.VMEM((2 * NB, LANES), jnp.float32),
            pltpu.VMEM((WIDTH, NB), jnp.float32),
        ],
        compiler_params=pltpu.CompilerParams(vmem_limit_bytes=60 * 1024 * 1024),
        name="factor_all",
    )(panels)


def solution(mesh):
    col_count = mesh.shape['col']
    block_spec = P(('batch', 'row'), 'col', None)
    own = PANELS // col_count

    def device_fn(a_local):
        local_rows, local_blocks, _ = a_local.shape
        local_tiles = local_rows // LANES
        col_rank = lax.axis_index('col')
        row_rank = lax.axis_index('row')
        share = a_local[:, :own, :].reshape(local_tiles, LANES, own, NB).transpose(2, 0, 3, 1)
        every = lax.all_gather(lax.all_gather(share, 'row'), 'col')
        panels = every.transpose(1, 3, 2, 0, 4, 5).reshape(-1, WIDTH, LANES)
        packed, _, t_factors, t_full = factor_all(panels)
        packed = lax.dynamic_slice_in_dim(packed, row_rank * local_tiles, local_tiles, 0)
        rows = row_rank * local_rows + jnp.arange(local_rows).reshape(local_tiles, 1, LANES)
        cols = jnp.arange(WIDTH).reshape(1, WIDTH, 1)
        refl = jnp.where(rows > cols, packed, jnp.where(rows == cols, 1.0, 0.0))
        refl = refl.transpose(1, 0, 2).reshape(WIDTH, local_rows)
        w_sum = lax.psum(jnp.einsum('kr,rbc->kbc', refl, a_local, precision=HIGHEST, preferred_element_type=jnp.float32), 'row')
        w_mat = jnp.einsum('kj,kbc->jbc', t_full, w_sum, precision=HIGHEST, preferred_element_type=jnp.float32)
        global_ids = jnp.arange(local_blocks) * col_count + col_rank
        w_mat = jnp.where((global_ids >= PANELS)[None, :, None], w_mat, 0.0)
        a_new = a_local - jnp.einsum('jr,jbc->rbc', refl, w_mat, precision=HIGHEST, preferred_element_type=jnp.float32)
        mine = packed.reshape(local_tiles, own, col_count, NB, LANES)
        mine = lax.dynamic_index_in_dim(mine, col_rank, 2, keepdims=False).transpose(0, 3, 1, 2).reshape(local_rows, own, NB)
        mine = jnp.pad(mine, ((0, 0), (0, local_blocks - own), (0, 0)))
        a_new = jnp.where((global_ids < PANELS)[None, :, None], mine, a_new)
        tau = jnp.diagonal(t_factors, axis1=1, axis2=2).reshape(-1)
        return a_new, tau, t_factors

    return jax.shard_map(device_fn, mesh=mesh, in_specs=(block_spec,), out_specs=(block_spec, P('batch'), P('batch', None, None)), check_vma=False)
```

time: 4100 us -> 788 us (0.19)
  blocking collectives: 1570 us -> 0 us
  loops' own time: 716 us -> 0 us
  matrix products: 685 us -> 179 us
  local copies, waits for them, and re-layouts: 519 us -> 151 us
  other arithmetic: 318 us -> 4.17 us
  Pallas kernels: 0 us -> 188 us
    psum x260 -> x0, blocking collectives: 1570 us -> none  [the longest x256 1530 us: column_step(): packed = lax.psum(packed, 'row')]
    another operation x4 -> x0, loops' own time: 716 us -> none  [factor_panel_rows(): lax.fori_loop(0, block_width, column_step, (panel_in, jnp.zeros((block_wi...]
    dot_general x312 -> x3, matrix products: 685 us -> 179 us  [the longest x1 83.2 us: device_fn(): jnp.einsum('jr,jbc->rbc', refl, w_mat, precision=HIGHEST, preferred_eleme...]
    select_n x1288 -> x0, other arithmetic: 290 us -> none  [the longest x256 190 us: apply_reflector(): refl_dot = jnp.where(col_ids > col_idx, refl_dot, 0.0)]
    dynamic_slice x768 -> x2, local copies, waits for them, and re-layouts: 315 us -> 33.5 us  [device_fn(): lax.dynamic_index_in_dim(mine, col_rank, 2, keepdims=False)]
    pallas_call x0 -> x1, Pallas kernels: none -> 188 us  [factor_all(): pl.pallas_call(factor_all_kernel, out_shape=(jax.ShapeDtypeStruct(panels....]
    psum x8 -> x1, waiting for transfers between devices: 249 us -> 109 us  [device_fn(): lax.psum(jnp.einsum('kr,rbc->kbc', refl, a_local, precision=HIGHEST, pref...]
    all_gather x0 -> x2, waiting for transfers between devices: none -> 138 us  [device_fn(): every = lax.all_gather(lax.all_gather(share, 'row'), 'col')]
  transfers between devices with their start and end apart: 8 -> 3, of which waited for: 7 -> 3; matrix products, arithmetic and copies ran while one was open for 2% -> 5% of each run, Pallas kernels for 0% -> 0%
where the time goes in v1:
time: 788 us; the launch traced here: 784 us
  waiting for transfers between devices  248 us (31%)
  Pallas kernels  188 us (24%)
  matrix products  179 us (23%)
  local copies, waits for them, and re-layouts  151 us (19%)
  between operations  14.1 us (2%)
    pallas_call x1, Pallas kernels, factor_all(): pl.pallas_call(factor_all_kernel, out_shape=(jax.ShapeDtypeStruct(panels....  188 us
    all_gather x2, waiting for transfers between devices, device_fn(): every = lax.all_gather(lax.all_gather(share, 'row'), 'col')  138 us
    psum x1, waiting for transfers between devices, device_fn(): lax.psum(jnp.einsum('kr,rbc->kbc', refl, a_local, precision=HIGHEST, pref...  109 us
    dot_general x1, matrix products, device_fn(): jnp.einsum('jr,jbc->rbc', refl, w_mat, precision=HIGHEST, preferred_eleme...  83.2 us
    dot_general x1, matrix products, device_fn(): jnp.einsum('kr,rbc->kbc', refl, a_local, precision=HIGHEST, preferred_ele...  78.4 us
    unnamed x5, local copies, waits for them, and re-layouts  56.8 us
    transpose x1, local copies, waits for them, and re-layouts, device_fn(): a_local[:, :own, :].reshape(local_tiles, LANES, own, NB)  46.1 us
    dynamic_slice x2, local copies, waits for them, and re-layouts, device_fn(): lax.dynamic_index_in_dim(mine, col_rank, 2, keepdims=False)  33.5 us
  transfers between devices with their start and end apart: 3, of which 3 were waited for; matrix products, arithmetic and copies ran while one was open for 5% of the time, Pallas kernels for 0%

profile of v1, /device:TPU:0, one launch (start us, length us, event | category | flops | bytes accessed | tf_op | source)
XLA Modules:
  0.0 784.3 jit_solution(14717585009683809322)
XLA Ops:
  7.2 0.0 all-gather.5.cloned.1.call-start
  7.2 46.1 %copy.29 = f32[2,16,64,128]{3,2,1,0:T(8,128)} copy(f32[2,16,64,128]{0,2,3,1:T(8,128)} %bitcast.2) | data formatting | bytes 2097152 | tf_op jit(solution)/shard_map/transpose | solution.py:264
  53.3 0.0 all-gather.5.cloned.1.call-update
  53.3 0.0 all-gather.7.cloned.1.call-start
  53.4 34.4 %all-gather.5.cloned.1.call-done = f32[8,16,64,128]{3,2,1,0:T(8,128)} async-done(((f32[2,16,64,128]{3,2,1,0:T(8,128)}), f32[8,16,64,128]{3,2,1,0:T(8,128)}) %all-gather.5.cloned.1.call-update) | async-done | bytes 4194320 | tf_op jit(solution)/shard_map/all_gather | solution.py:265
  87.8 0.0 all-gather.7.cloned.1.call-update
  87.8 0.0 all-reduce.3.cloned.1.call-start
  87.9 103.7 %all-gather.7.cloned.1.call-done = f32[8,2,16,64,128]{4,3,2,1,0:T(8,128)} async-done(((f32[4,2,16,64,128]{4,3,2,1,0:T(8,128)}), f32[8,2,16,64,128]{4,3,2,1,0:T(8,128)}) %all-gather.7.cloned.1.call-update) | async-done | bytes 8388624 | tf_op jit(solution)/shard_map/all_gather | solution.py:265
  191.6 8.3 %copy.30 = f32[4,16,2,2,64,128]{5,4,3,2,1,0:T(8,128)} copy(f32[4,16,2,2,64,128]{5,4,1,2,0,3:T(8,128)} %bitcast.40) | data formatting | bytes 16777216 | tf_op jit(solution)/shard_map/transpose | solution.py:266
  199.9 188.0 %factor_all.1 = (f32[64,256,128]{2,1,0:T(8,128)}, bf16[3,64,256,128]{3,2,1,0:T(8,128)(2,1)}, f32[4,64,64]{2,1,0:T(8,128)}, f32[256,256]{1,0:T(8,128)}) custom-call(f32[64,256,128]{2,1,0:T(8,128)} %bitcast.37), custom_call_target="tpu_custom_call" | custom-call | tf_op jit(solution)/shard_map/factor_all/pallas_call | solution.py:234
  387.8 4.1 select_bitcast_fusion
  392.0 1.9 copy.32
  393.9 78.4 %fusion = f32[256,128,64]{1,0,2:T(8,128)} fusion(f32[256,2048,1]{0,1,2:T(8,128)S(1)} %bitcast.38, f32[2048,128,64]{1,2,0:T(8,128)} %param.1), kind=kOutput, calls=%fused_computation.2 | convolution fusion | flops 51539607552 | bytes 77594624 | tf_op jit(solution)/shard_map/kr,rbc->kbc/dot_general | solution.py:273
  472.3 0.0 all-reduce.3.cloned.1.call-update
  472.4 1.3 constant_dynamic-slice_fusion
  473.7 32.2 %copy.31 = f32[16,2,1,64,128]{1,4,0,3,2:T(8,128)} copy(f32[16,2,1,64,128]{4,3,2,1,0:T(8,128)S(1)} %constant_dynamic-slice_fusion) | data formatting | bytes 2097152 | tf_op jit(solution)/shard_map/jit(dynamic_index_in_dim)/dynamic_slice | solution.py:279
  505.9 2.0 copy.38
  507.9 1.5 gather_fusion
  509.4 0.1 copy.39
  509.5 0.7 reshape.64
  510.1 109.5 %all-reduce.3.cloned.1.call-done = f32[256,128,64]{1,0,2:T(8,128)} async-done(((f32[256,128,64]{1,0,2:T(8,128)}), f32[256,128,64]{1,0,2:T(8,128)}) %all-reduce.3.cloned.1.call-update) | async-done | bytes 8388624 | tf_op jit(solution)/shard_map/psum | solution.py:273
  619.6 17.8 %fusion.6 = f32[128,64,256]{2,0,1:T(8,128)} fusion(f32[256,128,64]{1,0,2:T(8,128)} %all-reduce.3.cloned.1.call-done, f32[256,256]{1,0:T(8,128)S(1)} %copy-done), kind=kOutput, calls=%fused_computation.11 | convolution fusion | flops 6442450944 | bytes 17039360 | tf_op jit(solution)/shard_map/kj,kbc->jbc/dot_general | solution.py:274
  637.4 83.2 %subtract_select_fusion = f32[2048,128,64]{1,0,2:T(8,128)} fusion(f32[2048,2,64]{1,0,2:T(8,128)} %bitcast.10, f32[2048,128,64]{1,2,0:T(8,128)} %param.1, pred[128]{0:T(512)(128)(4,1)S(1)} %get-tuple-element.24, f32[256,2048,1]{0,1,2:T(8,128)S(1)} %bitcast.39, f32[128,64,256]{2,0,1:T(8,128)} %fusion.6, pred[128]{0:T(512)(128)(4,1)S(1)} %get-tuple-element.23), kind=kOutput, calls=%fused_computation.1 | convolution fusion | flops 51575259136 | bytes 145752320 | tf_op jit(solution)/shard_map/jr,jbc->rbc/dot_general | solution.py:277
  720.6 56.8 %copy.40 = f32[2048,128,64]{1,2,0:T(8,128)} copy(f32[2048,128,64]{1,0,2:T(8,128)} %subtract_select_fusion) | data formatting | bytes 134217728
  (7 shorter events, 0.0 us)
Async XLA Ops:
  7.2 80.7 %all-gather.5.cloned.1.call-start = ((), (), s32[]{:S(2)}) async-start(), calls=%async_computation.1 | async-start | bytes 5242880 | tf_op jit(solution)/shard_map/all_gather | solution.py:265
  53.3 138.3 %all-gather.7.cloned.1.call-start = ((), (), s32[]{:S(2)}) async-start(), calls=%async_computation.2 | async-start | bytes 12582912 | tf_op jit(solution)/shard_map/all_gather | solution.py:265
  87.8 531.8 %all-reduce.3.cloned.1.call-start = ((), (), s32[]{:S(2)}) async-start(), calls=%async_computation | async-start | bytes 16777216 | tf_op jit(solution)/shard_map/psum | solution.py:273
  473.7 32.2 %copy-start.1 = (f32[4,64,64]{2,1,0:T(8,128)S(1)}, f32[4,64,64]{2,1,0:T(8,128)}, u32[]{:S(2)}) copy-start(f32[4,64,64]{2,1,0:T(8,128)} %get-tuple-element.20) | copy-start | bytes 196612
  473.7 145.9 %copy-start = (f32[256,256]{1,0:T(8,128)S(1)}, f32[256,256]{1,0:T(8,128)}, u32[]{:S(2)}) copy-start(f32[256,256]{1,0:T(8,128)} %get-tuple-element.7) | copy-start | bytes 786436
Sparse Core Ops, SparseCore 0:
  53.4 34.3 all-gather.4
  89.3 102.2 all-gather.6
  472.5 147.1 all-reduce.2

commit v2 on v1

--- a/solution.py
+++ b/solution.py
@@ -251,35 +251,315 @@
     )(panels)
 
 
+PAIR = 2
+
+
+def refl_tile(packed, first_row):
+    rows = first_row + lax.broadcasted_iota(jnp.int32, packed.shape, 1)
+    cols = lax.broadcasted_iota(jnp.int32, packed.shape, 0)
+    return jnp.where(rows > cols, packed, jnp.where(rows == cols, 1.0, 0.0))
+
+
+def w_chunk(vt_ref, load_a, local_rows, k_block):
+    def body(kb, acc):
+        a = load_a(pl.multiple_of(kb * k_block, k_block), k_block)
+        high, mid, low = split3(a)
+        place = pl.ds(pl.multiple_of(kb * k_block, k_block), k_block)
+        full = jnp.dot(vt_ref[:, place], high, preferred_element_type=jnp.float32)
+        most = jnp.dot(vt_ref[: 2 * WIDTH, place], mid, preferred_element_type=jnp.float32)
+        least = jnp.dot(vt_ref[:WIDTH, place], low, preferred_element_type=jnp.float32)
+        small = (full[2 * WIDTH :] + least) + most[WIDTH:]
+        return acc + ((small + (full[WIDTH : 2 * WIDTH] + most[:WIDTH])) + full[:WIDTH])
+
+    return lax.fori_loop(0, local_rows // k_block, body, jnp.zeros((WIDTH, PAIR * LANES), jnp.float32))
+
+
+MESH = pl.DeviceIdType.MESH
+
+
+def reduce_kernel(a_ref, packed_ref, t_ref, w_ref, pk_buf, vt_ref, a_buf, ws_buf, wr_buf, wm_buf, wx_buf,
+                  pk_sem, a_sem, ws_send, ws_recv, wx_send, wx_recv, w2_send, w2_recv):
+    local_rows = a_ref.shape[0]
+    tiles = local_rows // LANES
+    pairs = a_ref.shape[1] // PAIR // 2
+    depth = a_buf.shape[0]
+    lag = 3
+    rank = lax.axis_index('row')
+    core = lax.rem(rank, 2)
+    partner = rank + 1 - 2 * core
+    across = lax.rem(rank + 2, 4)
+
+    barrier = pltpu.get_barrier_semaphore()
+    for peer in (partner, across):
+        pl.semaphore_signal(barrier, inc=1, device_id={'row': peer}, device_id_type=MESH)
+
+    pk_copy = pltpu.make_async_copy(packed_ref.at[pl.ds(rank * tiles, tiles)], pk_buf, pk_sem)
+    pk_copy.start()
+
+    def chunk_of(seq):
+        return seq - lax.rem(seq, 2) + lax.rem(seq + 1 + core, 2)
+
+    def fetch(seq, half):
+        slot = lax.rem(seq, depth)
+        return pltpu.make_async_copy(
+            a_ref.at[:, PAIR * chunk_of(seq) + half, :], a_buf.at[slot, half], a_sem.at[slot, half]
+        )
+
+    for seq in range(depth):
+        for half in range(PAIR):
+            fetch(seq, half).start()
+    pk_copy.wait()
+
+    def build(t, _):
+        v = refl_tile(pk_buf[t], rank * local_rows + t * LANES)
+        for s, part in enumerate(split3(v)):
+            vt_ref[pl.ds(s * WIDTH, WIDTH), pl.ds(pl.multiple_of(t * LANES, LANES), LANES)] = part
+        return 0
+
+    lax.fori_loop(0, tiles, build, 0)
+    pl.semaphore_wait(barrier, 2)
+
+    def partial_sum(seq):
+        slot = lax.rem(seq, depth)
+        for half in range(PAIR):
+            fetch(seq, half).wait()
+        a = jnp.concatenate([a_buf[slot, half] for half in range(PAIR)], axis=1)
+        high, mid, low = split3(a)
+        full = jnp.dot(vt_ref[...], high, preferred_element_type=jnp.float32)
+        most = jnp.dot(vt_ref[: 2 * WIDTH, :], mid, preferred_element_type=jnp.float32)
+        least = jnp.dot(vt_ref[:WIDTH, :], low, preferred_element_type=jnp.float32)
+        small = (full[2 * WIDTH :] + least) + most[WIDTH:]
+        return (small + (full[WIDTH : 2 * WIDTH] + most[:WIDTH])) + full[:WIDTH]
+
+    def refill(seq):
+        @pl.when(seq + depth < 2 * pairs)
+        def _():
+            for half in range(PAIR):
+                fetch(seq + depth, half).start()
+
+    def to_partner(i):
+        return pltpu.make_async_remote_copy(
+            src_ref=ws_buf.at[lax.rem(i, 2)], dst_ref=wr_buf.at[i], send_sem=ws_send.at[i], recv_sem=ws_recv.at[i],
+            device_id={'row': partner}, device_id_type=MESH,
+        )
+
+    def to_across(i):
+        return pltpu.make_async_remote_copy(
+            src_ref=wm_buf.at[i], dst_ref=wx_buf.at[i], send_sem=wx_send.at[i], recv_sem=wx_recv.at[i],
+            device_id={'row': across}, device_id_type=MESH,
+        )
+
+    def result(i, whose):
+        return pltpu.make_async_remote_copy(
+            src_ref=w_ref.at[2 * i + whose], dst_ref=w_ref.at[2 * i + whose], send_sem=w2_send.at[i],
+            recv_sem=w2_recv.at[i], device_id={'row': partner}, device_id_type=MESH,
+        )
+
+    def pair(i, _):
+        @pl.when(i < pairs)
+        def _():
+            theirs = partial_sum(2 * i)
+
+            @pl.when(i >= 2)
+            def _():
+                to_partner(i - 2).wait_send()
+
+            ws_buf[lax.rem(i, 2)] = theirs
+            refill(2 * i)
+            to_partner(i).start()
+            mine = partial_sum(2 * i + 1)
+            refill(2 * i + 1)
+            to_partner(i).wait_recv()
+            wm_buf[i] = mine + wr_buf[i]
+            to_across(i).start()
+
+        @pl.when(i >= lag)
+        def _():
+            j = i - lag
+            to_across(j).wait_recv()
+            w_ref[2 * j + core] = lax.dot_general(
+                t_ref[...], wm_buf[j] + wx_buf[j], (((0,), (0,)), ((), ())), precision=HIGHEST,
+                preferred_element_type=jnp.float32,
+            )
+            result(j, core).start()
+
+        return 0
+
+    lax.fori_loop(0, pairs + lag, pair, 0)
+    for i in (pairs - 2, pairs - 1):
+        to_partner(i).wait_send()
+
+    def drain(i, _):
+        to_across(i).wait_send()
+        result(i, core).wait_send()
+        result(i, 1 - core).wait_recv()
+        return 0
+
+    lax.fori_loop(0, pairs, drain, 0)
+
+
+def reduce_w(a3, packed, t_full):
+    local_rows, in_block, _ = a3.shape
+    tiles = local_rows // LANES
+    pairs = in_block // PAIR // 2
+    depth = 4
+    piece = (WIDTH, PAIR * LANES)
+    return pl.pallas_call(
+        reduce_kernel,
+        out_shape=jax.ShapeDtypeStruct((2 * pairs, *piece), jnp.float32),
+        in_specs=[pl.BlockSpec(memory_space=pl.ANY)] * 2 + [pl.BlockSpec(memory_space=pltpu.VMEM)],
+        out_specs=pl.BlockSpec(memory_space=pltpu.VMEM),
+        scratch_shapes=[
+            pltpu.VMEM((tiles, WIDTH, LANES), jnp.float32),
+            pltpu.VMEM((3 * WIDTH, local_rows), jnp.bfloat16),
+            pltpu.VMEM((depth, PAIR, local_rows, LANES), jnp.float32),
+            pltpu.VMEM((2, *piece), jnp.float32),
+            pltpu.VMEM((pairs, *piece), jnp.float32),
+            pltpu.VMEM((pairs, *piece), jnp.float32),
+            pltpu.VMEM((pairs, *piece), jnp.float32),
+            pltpu.SemaphoreType.DMA,
+            pltpu.SemaphoreType.DMA((depth, PAIR)),
+        ] + [pltpu.SemaphoreType.DMA((pairs,))] * 6,
+        compiler_params=pltpu.CompilerParams(
+            vmem_limit_bytes=56 * 1024 * 1024, collective_id=0, has_side_effects=True
+        ),
+        name="reduce_w",
+    )(a3, packed, t_full)
+
+
+def apply_kernel(row_rank_fn, col_rank_fn, col_count, a_ref, packed_ref, w_ref, o_ref,
+                 pk_buf, vr_ref, pt_ref, a_buf, w_buf, pk_sem, a_sem, w_sem, o_sem):
+    local_rows = a_ref.shape[0]
+    tiles = local_rows // LANES
+    chunks = a_ref.shape[1] // PAIR
+    depth = a_buf.shape[0]
+    ahead = depth - 2
+    own = PANELS // col_count
+    row_rank = row_rank_fn()
+    col_rank = col_rank_fn()
+    pk_copy = pltpu.make_async_copy(packed_ref.at[pl.ds(row_rank * tiles, tiles)], pk_buf, pk_sem)
+    pk_copy.start()
+
+    def fetch(i, half):
+        slot = lax.rem(i, depth)
+        return pltpu.make_async_copy(a_ref.at[:, PAIR * i + half, :], a_buf.at[slot, half], a_sem.at[slot, half])
+
+    def fetch_w(i):
+        slot = lax.rem(i, depth)
+        return pltpu.make_async_copy(w_ref.at[i], w_buf.at[slot], w_sem.at[slot])
+
+    def put(i, half):
+        slot = lax.rem(i, depth)
+        return pltpu.make_async_copy(a_buf.at[slot, half], o_ref.at[:, PAIR * i + half, :], o_sem.at[slot, half])
+
+    for i in range(ahead):
+        fetch_w(i).start()
+        for half in range(PAIR):
+            fetch(i, half).start()
+    pk_copy.wait()
+
+    def build(t, _):
+        place = pl.ds(pl.multiple_of(t * LANES, LANES), LANES)
+        packed = pk_buf[t]
+        v = refl_tile(packed, row_rank * local_rows + t * LANES).T
+        for s, part in enumerate(split3(v)):
+            vr_ref[place, s * WIDTH : (s + 1) * WIDTH] = part
+        mine = jnp.concatenate(
+            [pk_buf[t, pl.ds(pl.multiple_of((b * col_count + col_rank) * NB, NB), NB), :] for b in range(own)], axis=0
+        )
+        pt_ref[place, :] = mine.T
+        return 0
+
+    lax.fori_loop(0, tiles, build, 0)
+    m_block = 2048
+    lane = lax.broadcasted_iota(jnp.int32, (m_block, LANES), 1)
+
+    def chunk(i, _):
+        slot = lax.rem(i, depth)
+        fetch_w(i).wait()
+        for half in range(PAIR):
+            fetch(i, half).wait()
+        high, mid, low = split3(w_buf[slot])
+        rhs = jnp.concatenate([high, mid, low, high, mid, high], axis=0)
+
+        def body(mb, _):
+            rows = pl.ds(pl.multiple_of(mb * m_block, m_block), m_block)
+            vh, vm, vl = (vr_ref[rows, s * WIDTH : (s + 1) * WIDTH] for s in range(3))
+            lhs = jnp.concatenate([vh, vh, vh, vm, vm, vl], axis=1)
+            prod = jnp.dot(lhs, rhs, preferred_element_type=jnp.float32)
+            done = pt_ref[rows, :]
+            for half in range(PAIR):
+                new = a_buf[slot, half, rows, :] - prod[:, half * LANES : (half + 1) * LANES]
+                for b in range(own):
+                    shift = lax.rem(2 * LANES + b - b * NB - (PAIR * i + half), LANES)
+                    new = jnp.where(lane == b, pltpu.roll(done, shift, 1), new)
+                a_buf[slot, half, rows, :] = new
+            return 0
+
+        lax.fori_loop(0, local_rows // m_block, body, 0)
+        for half in range(PAIR):
+            put(i, half).start()
+
+        @pl.when(i + ahead < chunks)
+        def _():
+            @pl.when(i + ahead >= depth)
+            def _():
+                for half in range(PAIR):
+                    put(i + ahead - depth, half).wait()
+
+            fetch_w(i + ahead).start()
+            for half in range(PAIR):
+                fetch(i + ahead, half).start()
+
+        return 0
+
+    lax.fori_loop(0, chunks, chunk, 0)
+    for i in range(chunks - depth, chunks):
+        for half in range(PAIR):
+            put(i, half).wait()
+
+
+def apply_local(a3, packed, w, row_rank_fn, col_rank_fn, col_count):
+    local_rows, in_block, _ = a3.shape
+    tiles = local_rows // LANES
+    depth = 5
+    return pl.pallas_call(
+        lambda *refs: apply_kernel(row_rank_fn, col_rank_fn, col_count, *refs),
+        out_shape=jax.ShapeDtypeStruct(a3.shape, jnp.float32),
+        in_specs=[pl.BlockSpec(memory_space=pl.ANY)] * 3,
+        out_specs=pl.BlockSpec(memory_space=pl.ANY),
+        scratch_shapes=[
+            pltpu.VMEM((tiles, WIDTH, LANES), jnp.float32),
+            pltpu.VMEM((local_rows, 3 * WIDTH), jnp.bfloat16),
+            pltpu.VMEM((local_rows, LANES), jnp.float32),
+            pltpu.VMEM((depth, PAIR, local_rows, LANES), jnp.float32),
+            pltpu.VMEM((depth, WIDTH, PAIR * LANES), jnp.float32),
+            pltpu.SemaphoreType.DMA,
+            pltpu.SemaphoreType.DMA((depth, PAIR)),
+            pltpu.SemaphoreType.DMA((depth,)),
+            pltpu.SemaphoreType.DMA((depth, PAIR)),
+        ],
+        compiler_params=pltpu.CompilerParams(vmem_limit_bytes=56 * 1024 * 1024),
+        name="apply_local",
+    )(a3, packed, w)
+
+
 def solution(mesh):
     col_count = mesh.shape['col']
     block_spec = P(('batch', 'row'), 'col', None)
     own = PANELS // col_count
 
     def device_fn(a_local):
-        local_rows, local_blocks, _ = a_local.shape
+        local_rows, _, _ = a_local.shape
         local_tiles = local_rows // LANES
-        col_rank = lax.axis_index('col')
-        row_rank = lax.axis_index('row')
         share = a_local[:, :own, :].reshape(local_tiles, LANES, own, NB).transpose(2, 0, 3, 1)
         every = lax.all_gather(lax.all_gather(share, 'row'), 'col')
         panels = every.transpose(1, 3, 2, 0, 4, 5).reshape(-1, WIDTH, LANES)
         packed, _, t_factors, t_full = factor_all(panels)
-        packed = lax.dynamic_slice_in_dim(packed, row_rank * local_tiles, local_tiles, 0)
-        rows = row_rank * local_rows + jnp.arange(local_rows).reshape(local_tiles, 1, LANES)
-        cols = jnp.arange(WIDTH).reshape(1, WIDTH, 1)
-        refl = jnp.where(rows > cols, packed, jnp.where(rows == cols, 1.0, 0.0))
-        refl = refl.transpose(1, 0, 2).reshape(WIDTH, local_rows)
-        w_sum = lax.psum(jnp.einsum('kr,rbc->kbc', refl, a_local, precision=HIGHEST, preferred_element_type=jnp.float32), 'row')
-        w_mat = jnp.einsum('kj,kbc->jbc', t_full, w_sum, precision=HIGHEST, preferred_element_type=jnp.float32)
-        global_ids = jnp.arange(local_blocks) * col_count + col_rank
-        w_mat = jnp.where((global_ids >= PANELS)[None, :, None], w_mat, 0.0)
-        a_new = a_local - jnp.einsum('jr,jbc->rbc', refl, w_mat, precision=HIGHEST, preferred_element_type=jnp.float32)
-        mine = packed.reshape(local_tiles, own, col_count, NB, LANES)
-        mine = lax.dynamic_index_in_dim(mine, col_rank, 2, keepdims=False).transpose(0, 3, 1, 2).reshape(local_rows, own, NB)
-        mine = jnp.pad(mine, ((0, 0), (0, local_blocks - own), (0, 0)))
-        a_new = jnp.where((global_ids < PANELS)[None, :, None], mine, a_new)
+        a3 = a_local.transpose(0, 2, 1)
+        w_mat = reduce_w(a3, packed, t_full)
+        a_new = apply_local(a3, packed, w_mat, lambda: lax.axis_index('row'), lambda: lax.axis_index('col'), col_count)
         tau = jnp.diagonal(t_factors, axis1=1, axis2=2).reshape(-1)
-        return a_new, tau, t_factors
+        return a_new.transpose(0, 2, 1), tau, t_factors
 
     return jax.shard_map(device_fn, mesh=mesh, in_specs=(block_spec,), out_specs=(block_spec, P('batch'), P('batch', None, None)), check_vma=False)

time: 788 us -> 598 us (0.76)
  Pallas kernels: 188 us -> 388 us
  matrix products: 179 us -> 0 us
  waiting for transfers between devices: 248 us -> 138 us
  local copies, waits for them, and re-layouts: 151 us -> 56.7 us
    pallas_call x0 -> x2, Pallas kernels: none -> 201 us  [the longest x1 134 us: reduce_w(): pl.pallas_call(reduce_kernel, out_shape=jax.ShapeDtypeStruct((2 * pairs,...]
    dot_general x3 -> x0, matrix products: 179 us -> none  [the longest x1 83.2 us: device_fn(): jnp.einsum('jr,jbc->rbc', refl, w_mat, precision=HIGHEST, preferred_eleme...]
    psum x1 -> x0, waiting for transfers between devices: 109 us -> none  [device_fn(): lax.psum(jnp.einsum('kr,rbc->kbc', refl, a_local, precision=HIGHEST, pref...]
    unnamed x5 -> x2, local copies, waits for them, and re-layouts: 56.8 us -> 0.01 us
    dynamic_slice x2 -> x0, local copies, waits for them, and re-layouts: 33.5 us -> none  [device_fn(): lax.dynamic_index_in_dim(mine, col_rank, 2, keepdims=False)]
  transfers between devices with their start and end apart: 3 -> 2, of which waited for: 3 -> 2; matrix products, arithmetic and copies ran while one was open for 5% -> 0% of each run, Pallas kernels for 0% -> 0%
where the time goes in v2:
time: 598 us; the launch traced here: 597 us
  Pallas kernels  388 us (65%)
  waiting for transfers between devices  138 us (23%)
  local copies, waits for them, and re-layouts  56.7 us (9%)
  between operations  14.1 us (2%)
    pallas_call x1, Pallas kernels, factor_all(): pl.pallas_call(factor_all_kernel, out_shape=(jax.ShapeDtypeStruct(panels....  187 us
    all_gather x2, waiting for transfers between devices, device_fn(): every = lax.all_gather(lax.all_gather(share, 'row'), 'col')  138 us
    pallas_call x1, Pallas kernels, reduce_w(): pl.pallas_call(reduce_kernel, out_shape=jax.ShapeDtypeStruct((2 * pairs,...  134 us
    pallas_call x1, Pallas kernels, apply_local(): pl.pallas_call(lambda *refs: apply_kernel(row_rank_fn, col_rank_fn, col_c...  66.8 us
    transpose x1, local copies, waits for them, and re-layouts, device_fn(): a_local[:, :own, :].reshape(local_tiles, LANES, own, NB)  46.1 us
  transfers between devices with their start and end apart: 2, of which 2 were waited for; matrix products, arithmetic and copies ran while one was open for 0% of the time, Pallas kernels for 0%

profile of v2, /device:TPU:0, one launch (start us, length us, event | category | flops | bytes accessed | tf_op | source)
XLA Modules:
  0.0 597.1 jit_solution(12906918375877734603)
XLA Ops:
  7.2 0.0 all-gather.5.cloned.1.call-start
  7.2 46.1 %copy.14 = f32[2,16,64,128]{3,2,1,0:T(8,128)} copy(f32[2,16,64,128]{0,2,3,1:T(8,128)} %bitcast.3) | data formatting | bytes 2097152 | tf_op jit(solution)/shard_map/transpose | solution.py:555
  53.3 0.0 all-gather.5.cloned.1.call-update
  53.3 0.0 all-gather.7.cloned.1.call-start
  53.4 34.4 %all-gather.5.cloned.1.call-done = f32[8,16,64,128]{3,2,1,0:T(8,128)} async-done(((f32[2,16,64,128]{3,2,1,0:T(8,128)}), f32[8,16,64,128]{3,2,1,0:T(8,128)}) %all-gather.5.cloned.1.call-update) | async-done | bytes 4194320 | tf_op jit(solution)/shard_map/all_gather | solution.py:556
  87.8 0.0 all-gather.7.cloned.1.call-update
  87.9 103.8 %all-gather.7.cloned.1.call-done = f32[8,2,16,64,128]{4,3,2,1,0:T(8,128)} async-done(((f32[4,2,16,64,128]{4,3,2,1,0:T(8,128)}), f32[8,2,16,64,128]{4,3,2,1,0:T(8,128)}) %all-gather.7.cloned.1.call-update) | async-done | bytes 8388624 | tf_op jit(solution)/shard_map/all_gather | solution.py:556
  191.6 8.3 %copy.15 = f32[4,16,2,2,64,128]{5,4,3,2,1,0:T(8,128)} copy(f32[4,16,2,2,64,128]{5,4,1,2,0,3:T(8,128)} %bitcast.16) | data formatting | bytes 16777216 | tf_op jit(solution)/shard_map/transpose | solution.py:557
  199.9 187.4 %factor_all.1 = (f32[64,256,128]{2,1,0:T(8,128)}, bf16[3,64,256,128]{3,2,1,0:T(8,128)(2,1)}, f32[4,64,64]{2,1,0:T(8,128)}, f32[256,256]{1,0:T(8,128)}) custom-call(f32[64,256,128]{2,1,0:T(8,128)} %bitcast.15), custom_call_target="tpu_custom_call" | custom-call | tf_op jit(solution)/shard_map/factor_all/pallas_call | solution.py:234
  387.3 133.8 %reduce_w.1.refs_2_ = f32[32,256,256]{2,1,0:T(8,128)} custom-call(f32[2048,64,128]{2,1,0:T(8,128)} %bitcast.a_ref.refs_0_, f32[64,256,128]{2,1,0:T(8,128)} %get-tuple-element.6.packed_ref.refs_1_, f32[256,256]{1,0:T(8,128)} %get-tuple-element.7.t_ref), custom_call_target="tpu_custom_call" | custom-call | tf_op jit(solution)/shard_map/reduce_w/pallas_call | solution.py:407
  521.1 0.0 copy-start
  521.1 66.8 %apply_local.1 = f32[2048,64,128]{2,1,0:T(8,128)} custom-call(f32[2048,64,128]{2,1,0:T(8,128)} %bitcast.a_ref.refs_0_, f32[64,256,128]{2,1,0:T(8,128)} %get-tuple-element.6.packed_ref.refs_1_, f32[32,256,256]{2,1,0:T(8,128)} %reduce_w.1.refs_2_), custom_call_target="tpu_custom_call" | custom-call | tf_op jit(solution)/shard_map/apply_local/pallas_call | solution.py:526
  588.0 0.0 copy-done
  588.0 0.7 copy.16
  588.7 0.9 gather_fusion
  589.6 0.1 copy.17
  589.6 0.7 reshape.17
  (1 shorter events, 0.0 us)
Async XLA Ops:
  7.2 80.7 %all-gather.5.cloned.1.call-start = ((), (), s32[]{:S(2)}) async-start(), calls=%async_computation | async-start | bytes 5242880 | tf_op jit(solution)/shard_map/all_gather | solution.py:556
  53.3 138.3 %all-gather.7.cloned.1.call-start = ((), (), s32[]{:S(2)}) async-start(), calls=%async_computation.1 | async-start | bytes 12582912 | tf_op jit(solution)/shard_map/all_gather | solution.py:556
  521.1 66.9 %copy-start = (f32[4,64,64]{2,1,0:T(8,128)S(1)}, f32[4,64,64]{2,1,0:T(8,128)}, u32[]{:S(2)}) copy-start(f32[4,64,64]{2,1,0:T(8,128)} %get-tuple-element.5) | copy-start | bytes 196612
Sparse Core Ops, SparseCore 0:
  53.4 34.3 all-gather.4
  89.3 102.2 all-gather.6

commit v3 on v2

--- a/solution.py
+++ b/solution.py
@@ -427,6 +427,149 @@
     )(a3, packed, t_full)
 
 
+def gather_kernel(own, col_count, a_ref, out_ref, a_buf, a_sem, d_send, d_recv, x_send, x_recv, y_send, y_recv):
+    local_rows, in_block, _ = a_ref.shape
+    tiles = local_rows // LANES
+    depth = a_buf.shape[0]
+    pieces = x_send.shape[1]
+    piece_tiles = tiles // pieces
+    rank = lax.axis_index('row')
+    col = lax.axis_index('col')
+    core = lax.rem(rank, 2)
+    partner = rank + 1 - 2 * core
+    across = lax.rem(rank + 2, 4)
+    beside = 1 - col
+
+    barrier = pltpu.get_barrier_semaphore()
+    for peer in ({'row': partner}, {'row': across}, {'col': beside}):
+        pl.semaphore_signal(barrier, inc=1, device_id=peer, device_id_type=MESH)
+
+    def fetch(t):
+        slot = lax.rem(t, depth)
+        return pltpu.make_async_copy(a_ref.at[pl.ds(t * LANES, LANES)], a_buf.at[slot], a_sem.at[slot])
+
+    for t in range(depth):
+        fetch(t).start()
+
+    lane = lax.broadcasted_iota(jnp.int32, (8, LANES), 1)
+
+    def extract(t, _):
+        fetch(t).wait()
+        slot = lax.rem(t, depth)
+
+        def group(g, _):
+            outs = [jnp.zeros((8, LANES), jnp.float32)] * own
+            for r in range(LANES):
+                x = a_buf[slot, r, pl.ds(pl.multiple_of(8 * g, 8), 8), :]
+                outs = [
+                    jnp.where(lane == r, pltpu.roll(x, (r - b) % LANES, 1) if r != b else x, outs[b])
+                    for b in range(own)
+                ]
+            for b in range(own):
+                first = pl.multiple_of((b * col_count + col) * NB + 8 * g, 8)
+                out_ref[rank * tiles + t, pl.ds(first, 8), :] = outs[b]
+            return 0
+
+        lax.fori_loop(0, in_block // 8, group, 0)
+
+        @pl.when(t + depth < tiles)
+        def _():
+            fetch(t + depth).start()
+
+        return 0
+
+    def copy(row, column, b, piece, send, recv, peer):
+        where = out_ref.at[
+            pl.ds(row * tiles + piece * piece_tiles, piece_tiles),
+            pl.ds(pl.multiple_of((b * col_count + column) * NB, NB), NB),
+            :,
+        ]
+        return pltpu.make_async_remote_copy(
+            src_ref=where, dst_ref=where, send_sem=send, recv_sem=recv, device_id=peer, device_id_type=MESH
+        )
+
+    origins = ((rank, col), (across, col), (rank, beside), (across, beside))
+    across_p = lax.rem(partner + 2, 4)
+    origins_p = ((partner, col), (across_p, col), (partner, beside), (across_p, beside))
+
+    def to_partner(kind, b, piece, sending=True):
+        origin = (origins if sending else origins_p)[kind]
+        return copy(*origin, b, piece, d_send.at[kind, b, piece], d_recv.at[kind, b, piece], {'row': partner})
+
+    def over_x(kind, b, piece, sending=True):
+        origin = ((rank, col) if kind == 0 else (rank, beside)) if sending else ((across, col) if kind == 0 else (across, beside))
+        return copy(*origin, b, piece, x_send.at[kind * own + b, piece], x_recv.at[kind * own + b, piece], {'row': across})
+
+    def over_y(kind, b, piece, sending=True):
+        origin = ((rank, col) if kind == 0 else (across, col)) if sending else ((rank, beside) if kind == 0 else (across, beside))
+        return copy(*origin, b, piece, y_send.at[kind * own + b, piece], y_recv.at[kind * own + b, piece], {'col': beside})
+
+    def spread(piece):
+        for b in range(own):
+            over_x(0, b, piece).start()
+            over_y(0, b, piece).start()
+            to_partner(0, b, piece).start()
+
+    def forward(piece):
+        for b in range(own):
+            over_x(0, b, piece, False).wait_recv()
+            if b % 2:
+                over_y(1, b, piece).start()
+            to_partner(1, b, piece).start()
+            over_y(0, b, piece, False).wait_recv()
+            if b % 2 == 0:
+                over_x(1, b, piece).start()
+            to_partner(2, b, piece).start()
+
+    def last(piece):
+        for b in range(own):
+            (over_y if b % 2 else over_x)(1, b, piece, False).wait_recv()
+            to_partner(3, b, piece).start()
+
+    for piece in range(pieces):
+        lax.fori_loop(piece * piece_tiles, (piece + 1) * piece_tiles, extract, 0)
+        if piece == 0:
+            pl.semaphore_wait(barrier, 3)
+        spread(piece)
+        if piece:
+            forward(piece - 1)
+    forward(pieces - 1)
+    for piece in range(pieces):
+        last(piece)
+    for piece in range(pieces):
+        for b in range(own):
+            for kind in range(4):
+                to_partner(kind, b, piece).wait_send()
+                to_partner(kind, b, piece, False).wait_recv()
+            over_x(0, b, piece).wait_send()
+            over_y(0, b, piece).wait_send()
+            (over_y if b % 2 else over_x)(1, b, piece).wait_send()
+
+
+def gather_panels(a3, own, col_count, row_count):
+    local_rows, in_block, lanes = a3.shape
+    tiles = local_rows // LANES
+    depth = 3
+    pieces = 4
+    d_sems = pltpu.SemaphoreType.DMA((4, own, pieces))
+    link_sems = pltpu.SemaphoreType.DMA((2 * own, pieces))
+    return pl.pallas_call(
+        lambda *refs: gather_kernel(own, col_count, *refs),
+        out_shape=jax.ShapeDtypeStruct((row_count * tiles, WIDTH, LANES), jnp.float32),
+        in_specs=[pl.BlockSpec(memory_space=pl.ANY)],
+        out_specs=pl.BlockSpec(memory_space=pltpu.VMEM),
+        scratch_shapes=[
+            pltpu.VMEM((depth, LANES, in_block, lanes), jnp.float32),
+            pltpu.SemaphoreType.DMA((depth,)),
+            d_sems, d_sems, link_sems, link_sems, link_sems, link_sems,
+        ],
+        compiler_params=pltpu.CompilerParams(
+            vmem_limit_bytes=40 * 1024 * 1024, collective_id=1, has_side_effects=True
+        ),
+        name="gather_panels",
+    )(a3)
+
+
 def apply_kernel(row_rank_fn, col_rank_fn, col_count, a_ref, packed_ref, w_ref, o_ref,
                  pk_buf, vr_ref, pt_ref, a_buf, w_buf, pk_sem, a_sem, w_sem, o_sem):
     local_rows = a_ref.shape[0]
@@ -550,13 +693,9 @@
     own = PANELS // col_count
 
     def device_fn(a_local):
-        local_rows, _, _ = a_local.shape
-        local_tiles = local_rows // LANES
-        share = a_local[:, :own, :].reshape(local_tiles, LANES, own, NB).transpose(2, 0, 3, 1)
-        every = lax.all_gather(lax.all_gather(share, 'row'), 'col')
-        panels = every.transpose(1, 3, 2, 0, 4, 5).reshape(-1, WIDTH, LANES)
+        a3 = a_local.transpose(0, 2, 1)
+        panels = gather_panels(a3, own, col_count, mesh.shape['row'])
         packed, _, t_factors, t_full = factor_all(panels)
-        a3 = a_local.transpose(0, 2, 1)
         w_mat = reduce_w(a3, packed, t_full)
         a_new = apply_local(a3, packed, w_mat, lambda: lax.axis_index('row'), lambda: lax.axis_index('col'), col_count)
         tau = jnp.diagonal(t_factors, axis1=1, axis2=2).reshape(-1)

time: 598 us -> 458 us (0.77)
  waiting for transfers between devices: 138 us -> 0 us
  Pallas kernels: 388 us -> 452 us
  local copies, waits for them, and re-layouts: 56.7 us -> 5.54 us
  between operations: 14.1 us -> 0.69 us
    all_gather x2 -> x0, waiting for transfers between devices: 138 us -> none  [device_fn(): every = lax.all_gather(lax.all_gather(share, 'row'), 'col')]
    pallas_call x0 -> x1, Pallas kernels: none -> 63.2 us  [gather_panels(): pl.pallas_call(lambda *refs: gather_kernel(own, col_count, *refs), out_sh...]
    transpose x2 -> x0, local copies, waits for them, and re-layouts: 54.4 us -> none  [the longest x1 46.1 us: device_fn(): a_local[:, :own, :].reshape(local_tiles, LANES, own, NB)]
  transfers between devices with their start and end apart: 2 -> 0, of which waited for: 2 -> 0; matrix products, arithmetic and copies ran while one was open for 0% -> 0% of each run, Pallas kernels for 0% -> 0%
where the time goes in v3:
time: 458 us
  Pallas kernels  452 us (99%)
  local copies, waits for them, and re-layouts  5.54 us (1%)
    pallas_call x1, Pallas kernels, factor_all(): pl.pallas_call(factor_all_kernel, out_shape=(jax.ShapeDtypeStruct(panels....  187 us
    pallas_call x1, Pallas kernels, reduce_w(): pl.pallas_call(reduce_kernel, out_shape=jax.ShapeDtypeStruct((2 * pairs,...  134 us
    pallas_call x1, Pallas kernels, apply_local(): pl.pallas_call(lambda *refs: apply_kernel(row_rank_fn, col_rank_fn, col_c...  66.8 us
    pallas_call x1, Pallas kernels, gather_panels(): pl.pallas_call(lambda *refs: gather_kernel(own, col_count, *refs), out_sh...  63.2 us

profile of v3, /device:TPU:0, one launch (start us, length us, event | category | flops | bytes accessed | tf_op | source)
XLA Modules:
  0.0 458.0 jit_solution(7559326382113773855)
XLA Ops:
  0.6 63.2 %gather_panels.1.p_ref = f32[64,256,128]{2,1,0:T(8,128)S(1)} custom-call(f32[2048,64,128]{2,1,0:T(8,128)} %bitcast.refs_0_.a_ref), custom_call_target="tpu_custom_call" | custom-call | tf_op jit(solution)/shard_map/gather_panels/pallas_call | solution.py:556
  63.8 0.0 copy-start
  63.8 3.2 copy-done
  67.0 187.4 %factor_all.1 = (f32[64,256,128]{2,1,0:T(8,128)}, bf16[3,64,256,128]{3,2,1,0:T(8,128)(2,1)}, f32[4,64,64]{2,1,0:T(8,128)}, f32[256,256]{1,0:T(8,128)}) custom-call(f32[64,256,128]{2,1,0:T(8,128)} %copy-done), custom_call_target="tpu_custom_call" | custom-call | tf_op jit(solution)/shard_map/factor_all/pallas_call | solution.py:234
  254.4 134.4 %reduce_w.1.refs_2_ = f32[32,256,256]{2,1,0:T(8,128)} custom-call(f32[2048,64,128]{2,1,0:T(8,128)} %bitcast.refs_0_.a_ref, f32[64,256,128]{2,1,0:T(8,128)} %get-tuple-element.6.packed_ref.refs_1_, f32[256,256]{1,0:T(8,128)} %get-tuple-element.7.t_ref), custom_call_target="tpu_custom_call" | custom-call | tf_op jit(solution)/shard_map/reduce_w/pallas_call | solution.py:407
  388.8 0.0 copy-start.1
  388.8 66.8 %apply_local.1 = f32[2048,64,128]{2,1,0:T(8,128)} custom-call(f32[2048,64,128]{2,1,0:T(8,128)} %bitcast.refs_0_.a_ref, f32[64,256,128]{2,1,0:T(8,128)} %get-tuple-element.6.packed_ref.refs_1_, f32[32,256,256]{2,1,0:T(8,128)} %reduce_w.1.refs_2_), custom_call_target="tpu_custom_call" | custom-call | tf_op jit(solution)/shard_map/apply_local/pallas_call | solution.py:669
  455.6 0.0 copy-done.1
  455.6 0.7 copy.5
  456.3 0.9 gather_fusion
  457.2 0.1 copy.6
  457.3 0.7 reshape.9
  (1 shorter events, 0.0 us)
Async XLA Ops:
  63.8 3.2 copy-start
  388.8 66.9 %copy-start.1 = (f32[4,64,64]{2,1,0:T(8,128)S(1)}, f32[4,64,64]{2,1,0:T(8,128)}, u32[]{:S(2)}) copy-start(f32[4,64,64]{2,1,0:T(8,128)} %get-tuple-element.5) | copy-start | bytes 196612

commit v4 on v3

--- a/solution.py
+++ b/solution.py
@@ -6,6 +6,7 @@
 from jax.sharding import PartitionSpec as P
 
 NB = 64
+UNROLL = 31
 LANES = 128
 PANELS = 4
 WIDTH = NB * PANELS
@@ -96,28 +97,38 @@
             piv = [zero] * n_g
             accn = zero
             alf = zero
-            for t in range(n_tiles):
+            for t in range(2):
                 x = row(out_ref, j, t)
                 x1 = row(out_ref, j1, t)
-                if t < 2:
-                    rid = lane + t * LANES
-                    xm = jnp.where(rid > k, x, 0.0)
-                    pm = jnp.where(rid == k, 1.0, 0.0)
-                    x1 = x1 - h1 * xm - f1 * pm
-                    alf = alf + jnp.where(rid == k1, x1, 0.0)
-                    x1 = jnp.where(rid > k1, x1, 0.0)
-                else:
-                    x1 = x1 - h1 * x
+                rid = lane + t * LANES
+                xm = jnp.where(rid > k, x, 0.0)
+                pm = jnp.where(rid == k, 1.0, 0.0)
+                x1 = x1 - h1 * xm - f1 * pm
+                alf = alf + jnp.where(rid == k1, x1, 0.0)
+                x1 = jnp.where(rid > k1, x1, 0.0)
                 accn = accn + x1 * x1
                 for i in range(n_g):
                     a = out_ref[tile(g0 + i, t)]
-                    if t < 2:
-                        a = a - hs[i] * xm - fs[i] * pm
-                        piv[i] = piv[i] + jnp.where(rid == k1, a, 0.0)
-                    else:
-                        a = a - hs[i] * x
+                    a = a - hs[i] * xm - fs[i] * pm
+                    piv[i] = piv[i] + jnp.where(rid == k1, a, 0.0)
                     out_ref[tile(g0 + i, t)] = a
                     acc[i] = acc[i] + x1 * a
+
+            def some(c, sums):
+                accn, acc = sums
+                acc = list(acc)
+                for u in range(UNROLL):
+                    t = 2 + c * UNROLL + u
+                    x = row(out_ref, j, t)
+                    x1 = row(out_ref, j1, t) - h1 * x
+                    accn = accn + x1 * x1
+                    for i in range(n_g):
+                        a = out_ref[tile(g0 + i, t)] - hs[i] * x
+                        out_ref[tile(g0 + i, t)] = a
+                        acc[i] = acc[i] + x1 * a
+                return accn, acc
+
+            accn, acc = lax.fori_loop(0, (n_tiles - 2) // UNROLL, some, (accn, acc))
             return finish(acc, piv, accn, alf), coef
 
         carry, coef = lax.fori_loop(0, 8, step, (carry, [zero] * 3))
@@ -355,25 +366,31 @@
             recv_sem=w2_recv.at[i], device_id={'row': partner}, device_id_type=MESH,
         )
 
-    def pair(i, _):
-        @pl.when(i < pairs)
+    def step(seq, _):
+        i = seq // 2
+        first = lax.rem(seq, 2) == 0
+
+        @pl.when(seq < 2 * pairs)
         def _():
-            theirs = partial_sum(2 * i)
-
-            @pl.when(i >= 2)
+            part = partial_sum(seq)
+            refill(seq)
+
+            @pl.when(first)
             def _():
-                to_partner(i - 2).wait_send()
-
-            ws_buf[lax.rem(i, 2)] = theirs
-            refill(2 * i)
-            to_partner(i).start()
-            mine = partial_sum(2 * i + 1)
-            refill(2 * i + 1)
-            to_partner(i).wait_recv()
-            wm_buf[i] = mine + wr_buf[i]
-            to_across(i).start()
-
-        @pl.when(i >= lag)
+                @pl.when(i >= 2)
+                def _():
+                    to_partner(i - 2).wait_send()
+
+                ws_buf[lax.rem(i, 2)] = part
+                to_partner(i).start()
+
+            @pl.when(jnp.logical_not(first))
+            def _():
+                to_partner(i).wait_recv()
+                wm_buf[i] = part + wr_buf[i]
+                to_across(i).start()
+
+        @pl.when(jnp.logical_not(first) & (i >= lag))
         def _():
             j = i - lag
             to_across(j).wait_recv()
@@ -385,7 +402,7 @@
 
         return 0
 
-    lax.fori_loop(0, pairs + lag, pair, 0)
+    lax.fori_loop(0, 2 * (pairs + lag), step, 0)
     for i in (pairs - 2, pairs - 1):
         to_partner(i).wait_send()
 
@@ -550,7 +567,7 @@
     local_rows, in_block, lanes = a3.shape
     tiles = local_rows // LANES
     depth = 3
-    pieces = 4
+    pieces = 8
     d_sems = pltpu.SemaphoreType.DMA((4, own, pieces))
     link_sems = pltpu.SemaphoreType.DMA((2 * own, pieces))
     return pl.pallas_call(

time: 458 us -> 426 us (0.930)
  Pallas kernels: 452 us -> 419 us
    pallas_call x1, Pallas kernels: 134 us -> 107 us  [reduce_w(): pl.pallas_call(reduce_kernel, out_shape=jax.ShapeDtypeStruct((2 * pairs,...]
where the time goes in v4:
time: 426 us
  Pallas kernels  419 us (98%)
  local copies, waits for them, and re-layouts  5.54 us (1%)
    pallas_call x1, Pallas kernels, factor_all(): pl.pallas_call(factor_all_kernel, out_shape=(jax.ShapeDtypeStruct(panels....  185 us
    pallas_call x1, Pallas kernels, reduce_w(): pl.pallas_call(reduce_kernel, out_shape=jax.ShapeDtypeStruct((2 * pairs,...  107 us
    pallas_call x1, Pallas kernels, apply_local(): pl.pallas_call(lambda *refs: apply_kernel(row_rank_fn, col_rank_fn, col_c...  66.7 us
    pallas_call x1, Pallas kernels, gather_panels(): pl.pallas_call(lambda *refs: gather_kernel(own, col_count, *refs), out_sh...  60.3 us

profile of v4, /device:TPU:0, one launch (start us, length us, event | category | flops | bytes accessed | tf_op | source)
XLA Modules:
  0.0 425.6 jit_solution(3574968162988465417)
XLA Ops:
  0.6 60.3 %gather_panels.1.p_ref = f32[64,256,128]{2,1,0:T(8,128)S(1)} custom-call(f32[2048,64,128]{2,1,0:T(8,128)} %bitcast.refs_0_.a_ref), custom_call_target="tpu_custom_call" | custom-call | tf_op jit(solution)/shard_map/gather_panels/pallas_call | solution.py:573
  61.0 0.0 copy-start
  61.0 3.2 copy-done
  64.2 185.0 %factor_all.1 = (f32[64,256,128]{2,1,0:T(8,128)}, bf16[3,64,256,128]{3,2,1,0:T(8,128)(2,1)}, f32[4,64,64]{2,1,0:T(8,128)}, f32[256,256]{1,0:T(8,128)}) custom-call(f32[64,256,128]{2,1,0:T(8,128)} %copy-done), custom_call_target="tpu_custom_call" | custom-call | tf_op jit(solution)/shard_map/factor_all/pallas_call | solution.py:245
  249.2 107.2 %reduce_w.1.refs_2_ = f32[32,256,256]{2,1,0:T(8,128)} custom-call(f32[2048,64,128]{2,1,0:T(8,128)} %bitcast.refs_0_.a_ref, f32[64,256,128]{2,1,0:T(8,128)} %get-tuple-element.6.packed_ref.refs_1_, f32[256,256]{1,0:T(8,128)} %get-tuple-element.7.t_ref), custom_call_target="tpu_custom_call" | custom-call | tf_op jit(solution)/shard_map/reduce_w/pallas_call | solution.py:424
  356.5 0.0 copy-start.1
  356.5 66.7 %apply_local.1 = f32[2048,64,128]{2,1,0:T(8,128)} custom-call(f32[2048,64,128]{2,1,0:T(8,128)} %bitcast.refs_0_.a_ref, f32[64,256,128]{2,1,0:T(8,128)} %get-tuple-element.6.packed_ref.refs_1_, f32[32,256,256]{2,1,0:T(8,128)} %reduce_w.1.refs_2_), custom_call_target="tpu_custom_call" | custom-call | tf_op jit(solution)/shard_map/apply_local/pallas_call | solution.py:686
  423.2 0.0 copy-done.1
  423.2 0.7 copy.5
  423.9 0.9 gather_fusion
  424.8 0.1 copy.6
  424.9 0.7 reshape.9
  (1 shorter events, 0.0 us)
Async XLA Ops:
  61.0 3.2 copy-start
  356.5 66.8 %copy-start.1 = (f32[4,64,64]{2,1,0:T(8,128)S(1)}, f32[4,64,64]{2,1,0:T(8,128)}, u32[]{:S(2)}) copy-start(f32[4,64,64]{2,1,0:T(8,128)} %get-tuple-element.5) | copy-start | bytes 196612
